TPU v7x, 32 devices: a whole 2x2x4 slice. The times are simulated.
32 devices in a mesh: seq: 16 (over z, y, x), head: 2 (over core).
Axes of the slice: x: 2, y: 2, z: 4, core: 2. Of those that a mesh axis runs over, the one named last changes fastest.
Arguments:
- hidden_state: bfloat16 [8, 4096], replicated, may hold values from -18 to 18
- query_weight: bfloat16 [4096, 2, 2048], P('seq', 'head'), may hold values from -1 to 1
- up_key: bfloat16 [2, 256, 512], P('head'), may hold values from -1 to 1
- up_value: bfloat16 [2, 256, 512], P('head'), may hold values from -0.375 to 0.375
- latent_key: bfloat16 [8, 16384, 2, 256], P(None, 'seq', 'head'), may hold values from -256 to 256
- latent_value: bfloat16 [8, 16384, 2, 256], P(None, 'seq', 'head'), may hold values from -6 to 6
- lengths: int32 [8], replicated, may hold values from 12288 to 16384
- block_mask: int32 [8, 64], P(None, 'seq'), may hold values from 0 to 1, as said below
- out_weight: bfloat16 [2, 2048, 4096], P('head', 'seq'), may hold values from -0.09375 to 0.09375
Outputs:
- attn_out: float32 [8, 4096], replicated
Inputs may be any that keep to these rules, and one draw needn't show every extreme that they name: `block_mask`: blocks 0 and 32 of every sequence are valid.
All inputs are finite; a program needn't handle non-finite values.
Results may differ from a plain program's by a relative error of at most 0.0035.
Values sent between devices are 32-bit elements; how exact they have to be, the bound alone decides.
No kernel may reach another device: no remote copies, remote signals or barrier semaphores. Data moves between devices by JAX's collectives and lax.ppermute only.
A program may use at most 64 MiB of HBM per device.

v0:
```python
import math
import jax
import jax.numpy as jnp
from jax import lax
from jax.sharding import PartitionSpec as P

HD = 128
R = 256
BLOCK = 256
KPG = 4
REP = 4
QW = 2048


def joined(part, axis, combine):
    gathered = jax.tree.map(lambda a: lax.all_gather(a, axis), part)

    def take(source):
        return jax.tree.map(lambda a: lax.dynamic_index_in_dim(a, source, 0, False), gathered)

    return lax.fori_loop(
        1, lax.axis_size(axis), lambda source, state: combine(state, take(source)), take(0)
    )


def join_carries(earlier, later):
    peak_a, total_a, summed_a = earlier
    peak_b, total_b, summed_b = later
    peak = jnp.maximum(peak_a, peak_b)
    factor_a = jnp.exp(peak_a - peak)
    factor_b = jnp.exp(peak_b - peak)
    total = total_a * factor_a + total_b * factor_b
    summed = summed_a * factor_a[..., None] + summed_b * factor_b[..., None]
    return (peak, total, summed)


def body(
    hidden_state,
    query_weight,
    up_key,
    up_value,
    latent_key,
    latent_value,
    lengths,
    block_mask,
    out_weight,
):
    highest = lax.Precision.HIGHEST
    seq_index = lax.axis_index("seq")
    batch = hidden_state.shape[0]
    dim_rows = query_weight.shape[0]
    state_rows = lax.dynamic_slice_in_dim(hidden_state, seq_index * dim_rows, dim_rows, 1)
    partial_query = jnp.dot(state_rows, query_weight[:, 0, :], preferred_element_type=jnp.float32)
    query = lax.psum(partial_query, "seq")
    query_heads = query.reshape(batch, KPG, REP, HD)
    keys_lat = latent_key[:, :, 0, :]
    values_lat = latent_value[:, :, 0, :]
    context_len = keys_lat.shape[1]
    positions = seq_index * context_len + jnp.arange(context_len, dtype=jnp.int32)
    block_full = jnp.repeat(block_mask, BLOCK, axis=1)
    valid = (positions[None, :] < lengths[:, None]) & (block_full > 0)
    mask_heads = valid[:, None, None, :]
    scale = 1.0 / math.sqrt(HD)
    key_maps = up_key[0].astype(jnp.float32).reshape(R, KPG, HD)
    query_latent = jnp.einsum("bjrd,ejd->bjre", query_heads, key_maps, precision=highest)
    scores = (
        jnp.einsum("bjre,bce->bjrc", query_latent, keys_lat.astype(jnp.float32), precision=highest)
        * scale
    )
    peak = jnp.max(jnp.where(mask_heads, scores, -1e30), axis=-1)
    weights = jnp.where(mask_heads, jnp.exp(scores - peak[..., None]), 0.0)
    total = jnp.sum(weights, axis=-1)
    value_maps = up_value[0].astype(jnp.float32).reshape(R, KPG, HD)
    latent_sum = jnp.einsum(
        "bjrc,bce->bjre", weights, values_lat.astype(jnp.float32), precision=highest
    )
    summed = jnp.einsum("bjre,ejd->bjrd", latent_sum, value_maps, precision=highest)
    out_rows = out_weight.shape[1]
    peak_all, total_all, summed_all = joined((peak, total, summed), "seq", join_carries)
    context = (summed_all / total_all[..., None]).reshape(batch, QW).astype(jnp.bfloat16)
    context_rows = lax.dynamic_slice_in_dim(context, seq_index * out_rows, out_rows, 1)
    partial_out = jnp.dot(context_rows, out_weight[0], preferred_element_type=jnp.float32)
    return lax.psum(partial_out, ("seq", "head"))


def solution(mesh):
    in_specs = (
        P(),
        P("seq", "head", None),
        P("head", None, None),
        P("head", None, None),
        P(None, "seq", "head", None),
        P(None, "seq", "head", None),
        P(),
        P(None, "seq"),
        P("head", "seq", None),
    )
    out_specs = P()
    return jax.shard_map(body, mesh=mesh, in_specs=in_specs, out_specs=out_specs, check_vma=False)
```

profile of v0, /device:TPU:0, one launch (start us, length us, event | category | flops | bytes accessed | tf_op | source)
XLA Modules:
  0.0 361.0 jit_solution(18013315302296954894)
XLA Ops:
  6.5 1.6 fusion.13
  8.8 0.7 broadcast_compare_fusion
  9.6 0.7 compare_and_fusion
  10.3 1.0 reshape.54
  11.4 1.0 reshape.55
  12.4 106.7 %all-reduce.3.cloned.1.call-done = f32[8,4,4,128]{3,2,1,0:T(4,128)} async-done(((f32[8,4,4,128]{3,2,1,0:T(4,128)}), f32[8,4,4,128]{3,2,1,0:T(4,128)}) %all-reduce.3.cloned.1.call-update) | async-done | bytes 65552 | tf_op jit(solution)/shard_map/psum | solution.py:54
  119.1 1.4 convolution_bitcast_fusion
  120.4 5.7 %select_reduce_fusion = (f32[8,4,4]{2,1,0:T(4,128)S(1)}, f32[8,4,4,1024]{3,2,1,0:T(4,128)S(1)}) fusion(pred[8,1024]{1,0:T(8,128)(4,1)S(1)} %compare_and_fusion, f32[8,4,4,256]{3,2,1,0:T(4,128)S(1)} %convolution_bitcast_fusion, bf16[8,1024,1,256]{3,1,2,0:T(8,128)(2,1)} %param.15), kind=kOutput, calls=%fused_computation.22 | convolution fusion | flops 403046272 | bytes 4858368 | tf_op jit(solution)/shard_map/bjre,bce->bjrc/dot_general | solution.py:67
  126.1 2.1 fusion.4
  128.2 0.9 convolution_bitcast_fusion.1
  129.2 40.4 %all-gather = f32[128,4,4]{2,1,0:T(4,128)S(1)} all-gather(f32[8,4,4]{2,1,0:T(4,128)S(1)} %get-tuple-element.223), channel_id=2, replica_groups=mesh['seq'=16,'head'=2] {'seq'}, dimensions={0}, use_global_device_ids=true | all-gather | bytes 8704 | tf_op jit(solution)/shard_map/all_gather | solution.py:16
  170.6 37.1 %all-gather.1 = f32[128,4,4]{2,1,0:T(4,128)S(1)} all-gather(f32[8,4,4]{2,1,0:T(4,128)S(1)} %fusion.15), channel_id=3, replica_groups=mesh['seq'=16,'head'=2] {'seq'}, dimensions={0}, use_global_device_ids=true | all-gather | bytes 8704 | tf_op jit(solution)/shard_map/all_gather | solution.py:16
  208.4 0.8 slice.8
  209.2 20.1 %while.19 = (s32[]{:T(128)}, f32[8,4,4]{0,2,1:T(4,128)S(1)}, f32[8,4,4]{0,2,1:T(4,128)S(1)}, f32[8,4,4,128]{3,2,1,0:T(4,128)S(1)}, f32[16,8,4,4]{1,3,2,0:T(4,128...) while((s32[]{:T(128)}, f32[8,4,4]{0,2,1:T(4,128)S(1)}, ...), condition=%wide.region_4.5_spmd, body=%wide.region_3.4_spmd.sunk | while | flops 49925 | bytes 334991 | solution.py:21
  209.5 0.8 constant_dynamic-slice_fusion.2
  210.8 0.8 constant_dynamic-slice_fusion.2
  212.2 0.8 constant_dynamic-slice_fusion.2
  213.5 0.8 constant_dynamic-slice_fusion.2
  214.9 0.8 constant_dynamic-slice_fusion.2
  216.2 0.8 constant_dynamic-slice_fusion.2
  217.5 0.8 constant_dynamic-slice_fusion.2
  218.9 0.8 constant_dynamic-slice_fusion.2
  220.2 0.8 constant_dynamic-slice_fusion.2
  221.5 0.8 constant_dynamic-slice_fusion.2
  222.9 0.8 constant_dynamic-slice_fusion.2
  224.2 0.8 constant_dynamic-slice_fusion.2
  225.6 0.8 constant_dynamic-slice_fusion.2
  226.9 0.8 constant_dynamic-slice_fusion.2
  228.2 0.8 constant_dynamic-slice_fusion.2
  229.6 0.9 fusion.11
  230.5 122.4 %all-reduce.5.cloned.1.call-done = f32[8,4096]{1,0:T(8,128)} async-done(((f32[8,4096]{1,0:T(8,128)}), f32[8,4096]{1,0:T(8,128)}) %all-reduce.5.cloned.1.call-update) | async-done | bytes 131088 | tf_op jit(solution)/shard_map/psum | solution.py:83
  352.9 1.6 copy.84
  (85 shorter events, 9.8 us)
Async XLA Ops:
  6.5 223.1 %copy-start = (bf16[1,128,4096]{2,1,0:T(8,128)(2,1)S(1)}, bf16[1,128,4096]{2,1,0:T(8,128)(2,1)}, u32[]{:S(2)}) copy-start(bf16[1,128,4096]{2,1,0:T(8,128)(2,1)} %param.19) | copy-start | bytes 3145732
  6.5 112.5 %all-reduce.3.cloned.1.call-start = ((), (), s32[]{:S(2)}) async-start(), calls=%async_computation | async-start | bytes 131072 | tf_op jit(solution)/shard_map/psum | solution.py:54
  8.8 199.6 %all-gather.5.cloned.1.call-start = ((), (), s32[]{:S(2)}) async-start(), calls=%async_computation.2 | async-start | bytes 1114112 | tf_op jit(solution)/shard_map/all_gather | solution.py:16
  119.1 7.0 %copy-start.1 = (bf16[8,1024,1,256]{3,1,2,0:T(8,128)(2,1)S(1)}, bf16[8,1024,1,256]{3,1,2,0:T(8,128)(2,1)}, u32[]{:S(2)}) copy-start(bf16[8,1024,1,256]{3,1,2,0:T(8,128)(2,1)} %param.16) | copy-start | bytes 12582916
  129.2 223.8 %all-reduce.5.cloned.1.call-start = ((), (), s32[]{:S(2)}) async-start(), calls=%async_computation.1 | async-start | bytes 262144 | tf_op jit(solution)/shard_map/psum | solution.py:83
Sparse Core Ops, SparseCore 0:
  12.8 106.2 all-reduce.2
  129.3 55.2 all-gather.4
  230.7 122.2 all-reduce.4
where the time goes:
time: 362 us; the launch traced here: 361 us
  waiting for transfers between devices  229 us (63%)
  blocking collectives  77.6 us (21%)
  local copies, waits for them, and re-layouts  22.3 us (6%)
  between operations  13.2 us (4%)
  matrix products  12.6 us (3%)
  other arithmetic  5.93 us (2%)
    psum x1, waiting for transfers between devices, body(): return lax.psum(partial_out, ('seq', 'head'))  122 us
    psum x1, waiting for transfers between devices, body(): query = lax.psum(partial_query, 'seq')  107 us
    all_gather x2, blocking collectives, joined(): gathered = jax.tree.map(lambda a: lax.all_gather(a, axis), part)  77.6 us
    dynamic_slice x18, local copies, waits for them, and re-layouts, take(): lax.dynamic_index_in_dim(a, source, 0, False)  13.5 us
  transfers between devices with their start and end apart: 3, of which 2 were waited for; matrix products, arithmetic and copies ran while one was open for 1% of the time, Pallas kernels for 0%

commit v1 on v0

--- a/solution.py
+++ b/solution.py
@@ -51,7 +51,7 @@
     dim_rows = query_weight.shape[0]
     state_rows = lax.dynamic_slice_in_dim(hidden_state, seq_index * dim_rows, dim_rows, 1)
     partial_query = jnp.dot(state_rows, query_weight[:, 0, :], preferred_element_type=jnp.float32)
-    query = lax.psum(partial_query, "seq")
+    query = jnp.sum(lax.all_gather(partial_query, "seq"), axis=0)
     query_heads = query.reshape(batch, KPG, REP, HD)
     keys_lat = latent_key[:, :, 0, :]
     values_lat = latent_value[:, :, 0, :]

time: 362 us -> 311 us (0.86)
  waiting for transfers between devices: 229 us -> 178 us
    psum x1 -> x0, waiting for transfers between devices: 107 us -> none  [body(): query = lax.psum(partial_query, 'seq')]
    all_gather x0 -> x1, waiting for transfers between devices: none -> 55.6 us  [body(): query = jnp.sum(lax.all_gather(partial_query, 'seq'), axis=0)]
  transfers between devices with their start and end apart: 3 -> 3, of which waited for: 2 -> 2; matrix products, arithmetic and copies ran while one was open for 1% -> 2% of each run, Pallas kernels for 0% -> 0%
where the time goes in v1:
time: 311 us; the launch traced here: 310 us
  waiting for transfers between devices  178 us (57%)
  blocking collectives  77.3 us (25%)
  local copies, waits for them, and re-layouts  21.7 us (7%)
  between operations  13.2 us (4%)
  matrix products  12.4 us (4%)
  other arithmetic  7.2 us (2%)
    psum x1, waiting for transfers between devices, body(): return lax.psum(partial_out, ('seq', 'head'))  122 us
    all_gather x2, blocking collectives, joined(): gathered = jax.tree.map(lambda a: lax.all_gather(a, axis), part)  77.3 us
    all_gather x1, waiting for transfers between devices, body(): query = jnp.sum(lax.all_gather(partial_query, 'seq'), axis=0)  55.6 us
    dynamic_slice x18, local copies, waits for them, and re-layouts, take(): lax.dynamic_index_in_dim(a, source, 0, False)  13.5 us
  transfers between devices with their start and end apart: 3, of which 2 were waited for; matrix products, arithmetic and copies ran while one was open for 2% of the time, Pallas kernels for 0%

profile of v1, /device:TPU:0, one launch (start us, length us, event | category | flops | bytes accessed | tf_op | source)
XLA Modules:
  0.0 309.9 jit_solution(14213563821367820957)
XLA Ops:
  6.5 2.2 fusion.13
  8.8 1.0 reshape.54
  9.8 1.0 reshape.55
  10.9 0.7 broadcast_compare_fusion
  11.6 0.7 compare_and_fusion
  12.4 55.6 %all-gather.7.cloned.1.call-done = f32[128,2048]{1,0:T(8,128)} async-done(((f32[8,2048]{1,0:T(8,128)}), f32[128,2048]{1,0:T(8,128)}) %all-gather.7.cloned.1.call-update) | async-done | bytes 1048592 | tf_op jit(solution)/shard_map/all_gather | solution.py:54
  67.9 1.3 bitcast_reduce_fusion
  69.7 5.9 %select_reduce_fusion = (f32[8,4,4]{2,1,0:T(4,128)S(1)}, f32[8,4,4,1024]{3,2,1,0:T(4,128)S(1)}) fusion(pred[8,1024]{1,0:T(8,128)(4,1)S(1)} %compare_and_fusion, f32[8,4,4,256]{3,2,1,0:T(4,128)S(1)} %convolution_bitcast_fusion, bf16[8,1024,1,256]{3,1,2,0:T(8,128)(2,1)} %param.15), kind=kOutput, calls=%fused_computation.23 | convolution fusion | flops 403046272 | bytes 4858368 | tf_op jit(solution)/shard_map/bjre,bce->bjrc/dot_general | solution.py:67
  75.6 2.1 fusion.4
  77.6 0.9 convolution_bitcast_fusion.1
  78.7 40.0 %all-gather.1 = f32[128,4,4]{2,1,0:T(4,128)S(1)} all-gather(f32[8,4,4]{2,1,0:T(4,128)S(1)} %get-tuple-element.223), channel_id=3, replica_groups=mesh['seq'=16,'head'=2] {'seq'}, dimensions={0}, use_global_device_ids=true | all-gather | bytes 8704 | tf_op jit(solution)/shard_map/all_gather | solution.py:16
  119.6 37.3 %all-gather.2 = f32[128,4,4]{2,1,0:T(4,128)S(1)} all-gather(f32[8,4,4]{2,1,0:T(4,128)S(1)} %fusion.15), channel_id=4, replica_groups=mesh['seq'=16,'head'=2] {'seq'}, dimensions={0}, use_global_device_ids=true | all-gather | bytes 8704 | tf_op jit(solution)/shard_map/all_gather | solution.py:16
  157.5 0.8 slice.8
  158.4 20.1 %while.19 = (s32[]{:T(128)}, f32[8,4,4]{0,2,1:T(4,128)S(1)}, f32[8,4,4]{0,2,1:T(4,128)S(1)}, f32[8,4,4,128]{3,2,1,0:T(4,128)S(1)}, f32[16,8,4,4]{1,3,2,0:T(4,128...) while((s32[]{:T(128)}, f32[8,4,4]{0,2,1:T(4,128)S(1)}, ...), condition=%wide.region_4.5_spmd, body=%wide.region_3.4_spmd.sunk | while | flops 49925 | bytes 334991 | solution.py:21
  158.7 0.8 constant_dynamic-slice_fusion.2
  160.0 0.8 constant_dynamic-slice_fusion.2
  161.3 0.8 constant_dynamic-slice_fusion.2
  162.7 0.8 constant_dynamic-slice_fusion.2
  164.0 0.8 constant_dynamic-slice_fusion.2
  165.4 0.8 constant_dynamic-slice_fusion.2
  166.7 0.8 constant_dynamic-slice_fusion.2
  168.0 0.8 constant_dynamic-slice_fusion.2
  169.4 0.8 constant_dynamic-slice_fusion.2
  170.7 0.8 constant_dynamic-slice_fusion.2
  172.1 0.8 constant_dynamic-slice_fusion.2
  173.4 0.8 constant_dynamic-slice_fusion.2
  174.7 0.8 constant_dynamic-slice_fusion.2
  176.1 0.8 constant_dynamic-slice_fusion.2
  177.4 0.8 constant_dynamic-slice_fusion.2
  178.8 0.9 fusion.11
  179.7 122.1 %all-reduce.2.cloned.1.call-done = f32[8,4096]{1,0:T(8,128)} async-done(((f32[8,4096]{1,0:T(8,128)}), f32[8,4096]{1,0:T(8,128)}) %all-reduce.2.cloned.1.call-update) | async-done | bytes 131088 | tf_op jit(solution)/shard_map/psum | solution.py:83
  301.8 1.6 copy.82
  (86 shorter events, 9.6 us)
Async XLA Ops:
  6.5 172.2 %copy-start = (bf16[1,128,4096]{2,1,0:T(8,128)(2,1)S(1)}, bf16[1,128,4096]{2,1,0:T(8,128)(2,1)}, u32[]{:S(2)}) copy-start(bf16[1,128,4096]{2,1,0:T(8,128)(2,1)} %param.19) | copy-start | bytes 3145732
  6.5 61.4 %all-gather.7.cloned.1.call-start = ((), (), s32[]{:S(2)}) async-start(), calls=%async_computation.1 | async-start | bytes 1114112 | tf_op jit(solution)/shard_map/all_gather | solution.py:54
  8.8 148.8 %all-gather.9.cloned.1.call-start = ((), (), s32[]{:S(2)}) async-start(), calls=%async_computation.2 | async-start | bytes 1114112 | tf_op jit(solution)/shard_map/all_gather | solution.py:16
  69.3 6.3 %copy-start.1 = (bf16[8,1024,1,256]{3,1,2,0:T(8,128)(2,1)S(1)}, bf16[8,1024,1,256]{3,1,2,0:T(8,128)(2,1)}, u32[]{:S(2)}) copy-start(bf16[8,1024,1,256]{3,1,2,0:T(8,128)(2,1)} %param.16) | copy-start | bytes 12582916
  78.6 223.2 %all-reduce.2.cloned.1.call-start = ((), (), s32[]{:S(2)}) async-start(), calls=%async_computation | async-start | bytes 262144 | tf_op jit(solution)/shard_map/psum | solution.py:83
Sparse Core Ops, SparseCore 0:
  10.1 57.7 all-gather.6
  78.7 54.9 all-gather.8
  179.8 121.8 all-reduce.1

commit v2 on v0

--- a/solution.py
+++ b/solution.py
@@ -80,7 +80,7 @@
     context = (summed_all / total_all[..., None]).reshape(batch, QW).astype(jnp.bfloat16)
     context_rows = lax.dynamic_slice_in_dim(context, seq_index * out_rows, out_rows, 1)
     partial_out = jnp.dot(context_rows, out_weight[0], preferred_element_type=jnp.float32)
-    return lax.psum(partial_out, ("seq", "head"))
+    return jnp.sum(lax.all_gather(partial_out, ("seq", "head")), axis=0)
 
 
 def solution(mesh):

time: 362 us -> 301 us (0.83)
  waiting for transfers between devices: 229 us -> 166 us
    psum x1 -> x0, waiting for transfers between devices: 122 us -> none  [body(): return lax.psum(partial_out, ('seq', 'head'))]
    all_gather x0 -> x1, waiting for transfers between devices: none -> 59.6 us  [body(): return jnp.sum(lax.all_gather(partial_out, ('seq', 'head')), axis=0)]
  transfers between devices with their start and end apart: 3 -> 3, of which waited for: 2 -> 2; matrix products, arithmetic and copies ran while one was open for 1% -> 2% of each run, Pallas kernels for 0% -> 0%
where the time goes in v2:
time: 301 us; the launch traced here: 300 us
  waiting for transfers between devices  166 us (55%)
  blocking collectives  77.6 us (26%)
  local copies, waits for them, and re-layouts  20.7 us (7%)
  between operations  13.2 us (4%)
  matrix products  12.6 us (4%)
  other arithmetic  9 us (3%)
    psum x1, waiting for transfers between devices, body(): query = lax.psum(partial_query, 'seq')  107 us
    all_gather x2, blocking collectives, joined(): gathered = jax.tree.map(lambda a: lax.all_gather(a, axis), part)  77.6 us
    all_gather x1, waiting for transfers between devices, body(): return jnp.sum(lax.all_gather(partial_out, ('seq', 'head')), axis=0)  59.6 us
    dynamic_slice x18, local copies, waits for them, and re-layouts, take(): lax.dynamic_index_in_dim(a, source, 0, False)  13.5 us
  transfers between devices with their start and end apart: 3, of which 2 were waited for; matrix products, arithmetic and copies ran while one was open for 2% of the time, Pallas kernels for 0%

profile of v2, /device:TPU:0, one launch (start us, length us, event | category | flops | bytes accessed | tf_op | source)
XLA Modules:
  0.0 299.7 jit_solution(755139538395362622)
XLA Ops:
  6.5 1.6 fusion.13
  8.8 0.7 broadcast_compare_fusion
  9.6 0.7 compare_and_fusion
  10.3 1.0 reshape.54
  11.4 1.0 reshape.55
  12.4 106.7 %all-reduce.2.cloned.1.call-done = f32[8,4,4,128]{3,2,1,0:T(4,128)} async-done(((f32[8,4,4,128]{3,2,1,0:T(4,128)}), f32[8,4,4,128]{3,2,1,0:T(4,128)}) %all-reduce.2.cloned.1.call-update) | async-done | bytes 65552 | tf_op jit(solution)/shard_map/psum | solution.py:54
  119.1 1.4 convolution_bitcast_fusion
  120.4 5.7 %select_reduce_fusion = (f32[8,4,4]{2,1,0:T(4,128)S(1)}, f32[8,4,4,1024]{3,2,1,0:T(4,128)S(1)}) fusion(pred[8,1024]{1,0:T(8,128)(4,1)S(1)} %compare_and_fusion, f32[8,4,4,256]{3,2,1,0:T(4,128)S(1)} %convolution_bitcast_fusion, bf16[8,1024,1,256]{3,1,2,0:T(8,128)(2,1)} %param.15), kind=kOutput, calls=%fused_computation.23 | convolution fusion | flops 403046272 | bytes 4858368 | tf_op jit(solution)/shard_map/bjre,bce->bjrc/dot_general | solution.py:67
  126.1 2.1 fusion.4
  128.2 0.9 convolution_bitcast_fusion.1
  129.2 40.4 %all-gather = f32[128,4,4]{2,1,0:T(4,128)S(1)} all-gather(f32[8,4,4]{2,1,0:T(4,128)S(1)} %get-tuple-element.223), channel_id=2, replica_groups=mesh['seq'=16,'head'=2] {'seq'}, dimensions={0}, use_global_device_ids=true | all-gather | bytes 8704 | tf_op jit(solution)/shard_map/all_gather | solution.py:16
  170.6 37.1 %all-gather.1 = f32[128,4,4]{2,1,0:T(4,128)S(1)} all-gather(f32[8,4,4]{2,1,0:T(4,128)S(1)} %fusion.15), channel_id=3, replica_groups=mesh['seq'=16,'head'=2] {'seq'}, dimensions={0}, use_global_device_ids=true | all-gather | bytes 8704 | tf_op jit(solution)/shard_map/all_gather | solution.py:16
  208.4 0.8 slice.8
  209.2 20.1 %while.19 = (s32[]{:T(128)}, f32[8,4,4]{0,2,1:T(4,128)S(1)}, f32[8,4,4]{0,2,1:T(4,128)S(1)}, f32[8,4,4,128]{3,2,1,0:T(4,128)S(1)}, f32[16,8,4,4]{1,3,2,0:T(4,128...) while((s32[]{:T(128)}, f32[8,4,4]{0,2,1:T(4,128)S(1)}, ...), condition=%wide.region_4.5_spmd, body=%wide.region_3.4_spmd.sunk | while | flops 49925 | bytes 334991 | solution.py:21
  209.5 0.8 constant_dynamic-slice_fusion.2
  210.8 0.8 constant_dynamic-slice_fusion.2
  212.2 0.8 constant_dynamic-slice_fusion.2
  213.5 0.8 constant_dynamic-slice_fusion.2
  214.9 0.8 constant_dynamic-slice_fusion.2
  216.2 0.8 constant_dynamic-slice_fusion.2
  217.5 0.8 constant_dynamic-slice_fusion.2
  218.9 0.8 constant_dynamic-slice_fusion.2
  220.2 0.8 constant_dynamic-slice_fusion.2
  221.5 0.8 constant_dynamic-slice_fusion.2
  222.9 0.8 constant_dynamic-slice_fusion.2
  224.2 0.8 constant_dynamic-slice_fusion.2
  225.6 0.8 constant_dynamic-slice_fusion.2
  226.9 0.8 constant_dynamic-slice_fusion.2
  228.2 0.8 constant_dynamic-slice_fusion.2
  229.6 0.9 fusion.11
  230.5 59.6 %all-gather.9.cloned.1.call-done = f32[256,4096]{1,0:T(8,128)} async-done(((f32[8,4096]{1,0:T(8,128)}), f32[256,4096]{1,0:T(8,128)}) %all-gather.9.cloned.1.call-update) | async-done | bytes 4194320 | tf_op jit(solution)/shard_map/all_gather | solution.py:83
  290.1 3.0 %bitcast_reduce_fusion = f32[8,4096]{1,0:T(8,128)} fusion(f32[256,4096]{1,0:T(8,128)} %all-gather.9.cloned.1.call-done), kind=kLoop, calls=%fused_computation.14 | loop fusion | flops 1015808 | bytes 4325376 | tf_op jit(solution)/shard_map/reduce_sum | solution.py:83
  (85 shorter events, 9.8 us)
Async XLA Ops:
  6.5 223.1 %copy-start = (bf16[1,128,4096]{2,1,0:T(8,128)(2,1)S(1)}, bf16[1,128,4096]{2,1,0:T(8,128)(2,1)}, u32[]{:S(2)}) copy-start(bf16[1,128,4096]{2,1,0:T(8,128)(2,1)} %param.19) | copy-start | bytes 3145732
  6.5 112.5 %all-reduce.2.cloned.1.call-start = ((), (), s32[]{:S(2)}) async-start(), calls=%async_computation | async-start | bytes 131072 | tf_op jit(solution)/shard_map/psum | solution.py:54
  8.8 199.6 %all-gather.7.cloned.1.call-start = ((), (), s32[]{:S(2)}) async-start(), calls=%async_computation.1 | async-start | bytes 1114112 | tf_op jit(solution)/shard_map/all_gather | solution.py:16
  119.1 7.0 %copy-start.1 = (bf16[8,1024,1,256]{3,1,2,0:T(8,128)(2,1)S(1)}, bf16[8,1024,1,256]{3,1,2,0:T(8,128)(2,1)}, u32[]{:S(2)}) copy-start(bf16[8,1024,1,256]{3,1,2,0:T(8,128)(2,1)} %param.16) | copy-start | bytes 12582916
  129.2 161.0 %all-gather.9.cloned.1.call-start = ((), (), s32[]{:S(2)}) async-start(), calls=%async_computation.2 | async-start | bytes 4325376 | tf_op jit(solution)/shard_map/all_gather | solution.py:83
Sparse Core Ops, SparseCore 0:
  12.8 106.2 all-reduce.1
  129.3 55.2 all-gather.6
  230.7 59.4 all-gather.8
